TPU v7x, 32 devices: a whole 2x2x4 slice. The times are simulated.
32 devices in a mesh: row: 8 (over y, x, core), col: 4 (over z).
Axes of the slice: x: 2, y: 2, z: 4, core: 2. Of those that a mesh axis runs over, the one named last changes fastest.
Arguments:
- signal: float32 [128, 128, 16, 256], P('row', 'col'), may hold values from -40 to 40, as said below
- start_frames: float32 [256, 32], replicated, may hold values from -6 to 6
- start_sends: float32 [16, 8], replicated, may hold values from -6 to 6
- start_rows: float32 [128, 64], replicated, may hold values from -6 to 6
- start_cols: float32 [128, 64], replicated, may hold values from -6 to 6
- rank_frames: int32 [1], replicated, may hold values from 16 to 32
- rank_sends: int32 [1], replicated, may hold values from 4 to 8
Outputs:
- filtered: float32 [128, 128, 16, 256], P('row', 'col')
Inputs may be any that keep to these rules, and one draw needn't show every extreme that they name: `signal`: beamformed samples.
All inputs are finite; a program needn't handle non-finite values.
Results may differ from a plain program's by a relative error of at most 0.0003.
Values sent between devices are 32-bit elements; how exact they have to be, the bound alone decides.
No kernel may reach another device: no remote copies, remote signals or barrier semaphores. Data moves between devices by JAX's collectives and lax.ppermute only.
A program may use at most 128 MiB of HBM per device.

v0:
```python
import functools

import jax
import jax.numpy as jnp
from jax import lax
from jax.experimental import pallas as pl
from jax.experimental.pallas import tpu as pltpu
from jax.sharding import PartitionSpec as P


ITERS = 2
LANES = 128
SUB = 8
HIGH = lax.Precision.HIGHEST
F32 = jnp.float32
BF16 = jnp.bfloat16
VMEM = pltpu.VMEM


NN = (((1,), (0,)), ((), ()))
NT = (((1,), (1,)), ((), ()))
TN = (((0,), (0,)), ((), ()))


def mm(a, b, dims):
    return lax.dot_general(a, b, dims, preferred_element_type=F32)


def mmf(a, b, dims):
    return lax.dot_general(a, b, dims, precision=HIGH, preferred_element_type=F32)


def split2(x):
    hi = x.astype(BF16)
    return hi, (x - hi.astype(F32)).astype(BF16)


def iota(shape, dim):
    return lax.broadcasted_iota(jnp.int32, shape, dim)


def params(mib=24):
    return pltpu.CompilerParams(vmem_limit_bytes=mib * 2**20)


VSPEC = pl.BlockSpec(memory_space=VMEM)


def in_vmem(x):
    return pltpu.with_memory_space_constraint(x, VMEM)


def mm2(a, b, dims_last):
    (ah, al), (bh, bl) = a, b
    return mm(ah, bh, dims_last) + (mm(ah, bl, dims_last) + mm(al, bh, dims_last))


def pack(square):
    n = square.shape[0]
    h = n // 2
    top, low = square[:h], square[h:]
    row, lane = iota((h, n), 0), iota((h, n), 1)
    turned = pltpu.roll(low, h, 1)
    body = jnp.where(lane < row, turned, top)
    diag = jnp.sum(jnp.where(lane == row + h, low, 0.0), axis=0, keepdims=True)
    tail = jnp.where(iota((SUB, n), 0) == 0, jnp.broadcast_to(diag, (SUB, n)), 0.0)
    return body, tail


def unpack(body, tail):
    h, n = body.shape
    row, lane = iota((h, n), 0), iota((h, n), 1)
    flip = body.T
    first, last = flip[:h], flip[h:]
    if h % LANES:
        zeros = jnp.zeros((h, n - h), F32)
        first, last = jnp.concatenate([first, zeros], axis=1), jnp.concatenate([last, zeros], axis=1)
    else:
        first, last = jnp.concatenate([first, first], axis=1), jnp.concatenate([last, last], axis=1)
    top = jnp.where(lane < row, first, body)
    corner = pltpu.roll(jnp.where(lane < row, body, first), h, 1)
    corner = jnp.where(lane == row + h, jnp.broadcast_to(tail[:1], (h, n)), corner)
    return jnp.concatenate([top, jnp.where(lane < h, last, corner)], axis=0)


def gram_kernel(sends, block, ahead, x_ref, side_ref, col_ref, near_ref, mine_ref, other_ref, acc_frames, acc_sends, sems):
    frames = x_ref.shape[1]
    group = acc_sends.shape[0]
    steps = x_ref.shape[0] // block

    def copy(step):
        at = pl.ds(pl.multiple_of(step * block, block), block)
        return pltpu.make_async_copy(x_ref.at[at, :], near_ref.at[at, :], sems.at[step])

    for step in range(min(ahead, steps)):
        copy(step).start()
    acc_frames[...] = jnp.zeros_like(acc_frames)
    acc_sends[...] = jnp.zeros_like(acc_sends)

    def body(step, carry):
        copy(step).wait()

        @pl.when(step + ahead < steps)
        def _():
            copy(step + ahead).start()

        hi, lo = split2(near_ref[pl.ds(pl.multiple_of(step * block, block), block), :])
        acc_frames[...] += mm(hi, jnp.concatenate([hi, lo], axis=1), TN)
        total = acc_sends[...]
        for at in range(0, block, group):
            h, l = hi[at : at + group], lo[at : at + group]
            total += mm(h, jnp.concatenate([h, l], axis=0), NT)
        acc_sends[...] = total
        return carry

    lax.fori_loop(0, steps, body, 0)
    cross = acc_frames[:, frames:]
    body, tail = pack(acc_frames[:, :frames] + (cross + cross.T))
    cross = acc_sends[:, group:]
    pair = acc_sends[:, :group] + (cross + cross.T)
    same = iota(pair.shape, 0) // sends == iota(pair.shape, 1) // sends
    pair = jnp.where(same, pair, 0.0)
    folded = pair[:sends]
    for at in range(sends, group, sends):
        folded = folded + pair[at : at + sends]
    half = sends // 2
    pick = (iota((group, LANES), 0) % sends == iota((group, LANES), 1)).astype(F32)
    small = mmf(folded, pick, NN)
    small = small[:half] + pltpu.roll(small[half:], sends, 1)
    side = side_ref[0]
    for ref, at in ((mine_ref, side), (other_ref, 1 - side)):
        left = at == 0
        ref[: body.shape[0]] = jnp.where(left, body[:, :LANES], body[:, LANES:])
        ref[body.shape[0] :] = jnp.where(left, tail[:, :LANES] + small, tail[:, LANES:])


def signal_grams(flat, sends, side, col):
    rows, frames = flat.shape
    block = min(rows, 1024)
    shape = (frames // 2 + SUB, LANES)
    return pl.pallas_call(
        functools.partial(gram_kernel, sends, block, 3),
        in_specs=[pl.BlockSpec(memory_space=pltpu.HBM)] + [pl.BlockSpec(memory_space=pltpu.SMEM)] * 2,
        out_specs=[VSPEC] * 3,
        out_shape=[VMEM(flat.shape, F32)] + [jax.ShapeDtypeStruct(shape, F32)] * 2,
        scratch_shapes=[
            VMEM((frames, 2 * frames), F32),
            VMEM((LANES, 2 * LANES), F32),
            pltpu.SemaphoreType.DMA((rows // block,)),
        ],
        compiler_params=params(),
        name="signal_grams",
    )(pltpu.with_memory_space_constraint(flat, pltpu.HBM), side, col)


def sweep(inner, image):
    count = inner.shape[0]
    blocks = count // SUB
    tiles = image.shape[1] // LANES
    a = [inner[SUB * i : SUB * (i + 1)] for i in range(blocks)]
    z = [
        [image[SUB * i : SUB * (i + 1), LANES * t : LANES * (t + 1)] for t in range(tiles)]
        for i in range(blocks)
    ]
    row = iota((SUB, LANES), 0)
    done = []
    for j in range(blocks):
        cols = [
            {i: jnp.broadcast_to(a[i][:, SUB * j + k : SUB * j + k + 1], (SUB, LANES)) for i in range(j, blocks)}
            for k in range(SUB)
        ]
        scale = jnp.zeros((SUB, LANES), F32)
        for k in range(SUB):
            pivot = jnp.broadcast_to(cols[k][j][k : k + 1], (SUB, LANES))
            inverse = 1.0 / pivot
            scale = jnp.where(row == k, lax.rsqrt(pivot), scale)
            a_row = jnp.broadcast_to(a[j][k : k + 1], (SUB, LANES)) * inverse
            z_row = [jnp.broadcast_to(t[k : k + 1], (SUB, LANES)) * inverse for t in z[j]]
            c_row = {
                q: jnp.broadcast_to(cols[q][j][k : k + 1], (SUB, LANES)) * inverse for q in range(k + 1, SUB)
            }
            for i in range(j, blocks):
                by = cols[k][i]
                if i == j:
                    by = jnp.where(row > k, by, 0.0)
                for q in range(k + 1, SUB):
                    cols[q][i] = cols[q][i] - by * c_row[q]
                if j + 1 < blocks:
                    a[i] = a[i] - by * a_row
                z[i] = [t - by * r for t, r in zip(z[i], z_row)]
        done.append([t * scale for t in z[j]])
    lines = [jnp.concatenate(d, axis=1) if tiles > 1 else d[0] for d in done]
    return jnp.concatenate(lines, axis=0) if blocks > 1 else lines[0]


def orthonormal(gram, start):
    def body(_, basis):
        image = mmf(basis, gram, NN)
        count = image.shape[0]
        padded = jnp.concatenate([image, jnp.zeros((LANES - count, image.shape[1]), F32)], axis=0)
        return sweep(mmf(image, padded, NT), image)

    return lax.fori_loop(0, ITERS, body, start)


def small_bases_kernel(
    kmax, cols, sends, mine_ref, other_ref, side_ref, sf_ref, ss_ref, rf_ref, rs_ref, frames_ref, spread_ref
):
    h = mine_ref.shape[0] - SUB
    left = side_ref[0] == 0
    mine, other = mine_ref[...], other_ref[...]
    first, last = jnp.where(left, mine, other), jnp.where(left, other, mine)
    gram_f = unpack(jnp.concatenate([first[:h], last[:h]], axis=1), jnp.concatenate([first[h:], last[h:]], axis=1))
    small = first[h:]
    lane = iota(small.shape, 1)
    gram_s = jnp.concatenate(
        [
            jnp.where(lane < sends, small, 0.0),
            jnp.where(lane < sends, pltpu.roll(small, LANES - sends, 1), 0.0),
            jnp.zeros((LANES - sends, LANES), F32),
        ],
        axis=0,
    )

    def body(_, bases):
        images = [mmf(basis, gram, NN) for basis, gram in zip(bases, (gram_f, gram_s))]
        inners = [
            mmf(i, jnp.concatenate([i, jnp.zeros((LANES - i.shape[0], i.shape[1]), F32)], axis=0), NT) for i in images
        ]
        return tuple(sweep(n, i) for n, i in zip(inners, images))

    basis_f, basis_s = lax.fori_loop(0, ITERS, body, (sf_ref[...], ss_ref[...]))
    frames_ref[...] = jnp.where(iota(basis_f.shape, 0) < rf_ref[0], basis_f, 0.0)
    basis_s = jnp.where(iota(basis_s.shape, 0) < rs_ref[0], basis_s, 0.0)
    pick = (iota((kmax, kmax * cols), 0) == iota((kmax, kmax * cols), 1) // cols).astype(F32)
    spread_ref[...] = mmf(basis_s, pick, TN)[:sends]


def small_bases(mine, other, side, start_frames, start_sends, rank_frames, rank_sends, cols):
    frames, tmax = start_frames.shape
    sends, kmax = start_sends.shape
    padded = jnp.pad(start_sends.T, ((0, 0), (0, LANES - sends)))
    smem = pl.BlockSpec(memory_space=pltpu.SMEM)
    return pl.pallas_call(
        functools.partial(small_bases_kernel, kmax, cols, sends),
        in_specs=[VSPEC, VSPEC, smem, VSPEC, VSPEC, smem, smem],
        out_specs=[VSPEC, VSPEC],
        out_shape=[jax.ShapeDtypeStruct((tmax, frames), F32), jax.ShapeDtypeStruct((sends, kmax * cols), F32)],
        compiler_params=params(),
        name="small_bases",
    )(mine, other, side, start_frames.T, padded, rank_frames, rank_sends)


def mixing(spread, cols):
    sends, wide = spread.shape
    tall = jnp.broadcast_to(spread[None], (cols, sends, wide)).reshape(cols * sends, wide)
    same = iota(tall.shape, 0) // sends == iota(tall.shape, 1) % cols
    return jnp.where(same, tall, 0.0)


def core_kernel(lanes, cols, per, x_ref, basis_ref, spread_ref, out_ref, held, mix_ref):
    tmax = basis_ref.shape[0]
    mix_ref[0], mix_ref[1] = split2(mixing(spread_ref[...], cols))
    bh, bl = split2(basis_ref[...])
    base = jnp.concatenate([bh, bl], axis=0)
    span = mix_ref.shape[1]

    def body(step, carry):
        his, los = [], []
        for q in range(per):
            at = pl.multiple_of((step * per + q) * span, span)
            xh, xl = split2(x_ref[pl.ds(at, span), :])
            both = mm(base, xh, NT)
            h, l = split2(both[:tmax] + (both[tmax:] + mm(bh, xl, NT)))
            his.append(h)
            los.append(l)
        rows = per * tmax
        stack = jnp.concatenate(his + los, axis=0)
        both = mm(stack, mix_ref[0], NN)
        c = both[:rows] + (both[rows:] + mm(stack[:rows], mix_ref[1], NN))
        for q in range(per):
            for h in range(c.shape[1] // lanes):
                held[step * per + q, h * tmax : (h + 1) * tmax] = c[
                    q * tmax : (q + 1) * tmax, h * lanes : (h + 1) * lanes
                ]
        return carry

    lax.fori_loop(0, held.shape[0] // per, body, 0)
    for r in range(held.shape[0]):
        out_ref[:, r, :] = held[r]


def project(flat, basis, spread, rows_dev, cols, lanes):
    tmax = basis.shape[0]
    sends, wide = spread.shape
    span = cols * sends
    per = 2 if rows_dev % 2 == 0 else 1
    high = wide * tmax // lanes
    return pl.pallas_call(
        functools.partial(core_kernel, lanes, cols, per),
        in_specs=[VSPEC] * 3,
        out_specs=VSPEC,
        out_shape=VMEM((high, rows_dev, lanes), F32),
        scratch_shapes=[VMEM((rows_dev, high, lanes), F32), VMEM((2, span, wide), BF16)],
        compiler_params=params(),
        name="project",
    )(flat, basis, spread)


def block_of(ref, j, g):
    part = ref[:, j, g]
    return part.reshape(part.shape[0] * part.shape[1], part.shape[2])


def row_gram_kernel(m_ref, col_ref, out_ref, *piece_refs):
    sections = m_ref.shape[1]
    for by, piece_ref in enumerate(piece_refs):
        to = lax.rem(col_ref[0] + by, sections)
        for i in range(m_ref.shape[0]):
            for g in range(m_ref.shape[2]):
                piece_ref[i, g] = m_ref[i, to, g]
    total = None
    cross = None
    for j in range(m_ref.shape[1]):
        for g in range(m_ref.shape[2]):
            h, l = split2(block_of(m_ref, j, g))
            hh, hl = mm(h, h, NT), mm(h, l, NT)
            total = hh if total is None else total + hh
            cross = hl if cross is None else cross + hl
    put(out_ref, total + (cross + cross.T))


def put(ref, square):
    body, tail = pack(square)
    ref[: body.shape[0]] = body
    ref[body.shape[0] :] = tail


def get(ref):
    h = ref.shape[0] - SUB
    return unpack(ref[:h], ref[h:])


def row_gram(m, col):
    rows = m.shape[0] * m.shape[3]
    piece = jax.ShapeDtypeStruct((m.shape[0],) + m.shape[2:], F32)
    sections = m.shape[1]
    return pl.pallas_call(
        row_gram_kernel,
        in_specs=[VSPEC, pl.BlockSpec(memory_space=pltpu.SMEM)],
        out_specs=[VSPEC] * (1 + sections),
        out_shape=[jax.ShapeDtypeStruct((rows // 2 + SUB, rows), F32)] + [piece] * sections,
        compiler_params=params(),
        name="row_gram",
    )(m, col)


def second_kernel(cols, gram_ref, start_ref, col_ref, *refs):
    piece_refs = refs[:-3]
    basis_ref, second_ref, out_ref = refs[-3:]
    basis = orthonormal(get(gram_ref), start_ref[...])
    basis_ref[...] = basis
    uh, ul = split2(basis)
    twice = jnp.concatenate([uh, uh], axis=1)
    sections = len(piece_refs)
    low = piece_refs[0].shape[3] // cols
    total = None
    cross = None
    contract = (((0,), (1,)), ((), ()))
    for g in range(piece_refs[0].shape[1]):
        for by, piece_ref in enumerate(piece_refs):
            at = pl.multiple_of(lax.rem(col_ref[0] + (sections - by), sections) * cols, cols)
            part = piece_ref[:, g]
            h, l = split2(part.reshape(part.shape[0] * part.shape[1], part.shape[2]))
            t = mm(jnp.concatenate([h, l], axis=0), twice, contract) + mm(h, ul, contract)
            for e in range(low):
                second_ref[g * low + e, pl.ds(at, cols)] = t[e * cols : (e + 1) * cols]
        for e in range(low):
            h, l = split2(second_ref[g * low + e])
            hh, hl = mm(h, h, NT), mm(h, l, NT)
            total = hh if total is None else total + hh
            cross = hl if cross is None else cross + hl
    put(out_ref, total + (cross + cross.T))


def second_stage(gram, start, col, pieces, cols):
    rows, kept = start.shape
    sections, groups, lanes = len(pieces), pieces[0].shape[1], pieces[0].shape[3]
    low = lanes // cols
    wide = sections * cols
    return pl.pallas_call(
        functools.partial(second_kernel, cols),
        in_specs=[VSPEC, VSPEC, pl.BlockSpec(memory_space=pltpu.SMEM)] + [VSPEC] * sections,
        out_specs=[VSPEC] * 3,
        out_shape=[
            jax.ShapeDtypeStruct((kept, rows), F32),
            jax.ShapeDtypeStruct((groups * low, wide, kept), F32),
            jax.ShapeDtypeStruct((wide // 2 + SUB, wide), F32),
        ],
        compiler_params=params(),
        name="second_stage",
    )(gram, start.T, col, *pieces)


def third_kernel(cols, gram_ref, start_ref, basis_ref, second_ref, out_ref):
    basis_c = orthonormal(get(gram_ref), start_ref[...])
    ph, pl_ = split2(mmf(basis_c, basis_c, TN))
    twice = jnp.concatenate([ph, ph], axis=1)
    rows_t = split2(basis_ref[...].T)
    sections = out_ref.shape[1]
    low = out_ref.shape[4] // cols
    for g in range(out_ref.shape[2]):
        kept = []
        for e in range(low):
            h, l = split2(second_ref[g * low + e])
            kept.append(split2(mm(twice, jnp.concatenate([h, l], axis=0), NN) + mm(pl_, h, NN)))
        for j in range(sections):
            part = [
                jnp.concatenate([k[w][j * cols : (j + 1) * cols] for k in kept], axis=0) for w in range(2)
            ]
            t = mm2(rows_t, part, NT)
            out_ref[:, j, g] = t.reshape(out_ref.shape[0], out_ref.shape[3], out_ref.shape[4])


def third_stage(gram, start, basis, second, shape, cols):
    return pl.pallas_call(
        functools.partial(third_kernel, cols),
        in_specs=[VSPEC] * 4,
        out_specs=VSPEC,
        out_shape=VMEM(shape, F32),
        compiler_params=params(),
        name="third_stage",
    )(gram, start.T, basis, second)


def expand_kernel(cols, per, x_ref, t_ref, basis_ref, spread_ref, out_ref, held, mix_ref, base_ref):
    step = pl.program_id(0)
    tmax = basis_ref.shape[0]

    @pl.when(step == 0)
    def _():
        hi, lo = split2(mixing(spread_ref[...], cols))
        mix_ref[0], mix_ref[1] = hi.T, lo.T
        hi, lo = split2(basis_ref[...])
        for q, part in enumerate((hi, lo, hi)):
            base_ref[q * tmax : (q + 1) * tmax] = part
        for r in range(held.shape[0]):
            held[r] = t_ref[:, r, :]

    span = mix_ref.shape[2]
    tiles = []
    for q in range(per):
        t = held[step * per + q]
        tiles.append(jnp.concatenate([t[h * tmax : (h + 1) * tmax] for h in range(t.shape[0] // tmax)], axis=1))
    hi, lo = split2(jnp.concatenate(tiles, axis=0))
    rows = per * tmax
    both = mm(jnp.concatenate([hi, lo], axis=0), mix_ref[0], NN)
    zh, zl = split2(both[:rows] + (both[rows:] + mm(hi, mix_ref[1], NN)))
    for q in range(per):
        h, l = zh[q * tmax : (q + 1) * tmax], zl[q * tmax : (q + 1) * tmax]
        tissue = mm(jnp.concatenate([h, h, l], axis=0), base_ref[...], TN)
        at = pl.multiple_of((step * per + q) * span, span)
        out_ref[q * span : (q + 1) * span] = x_ref[pl.ds(at, span), :] - tissue


def expand(flat, t, basis, spread, cols):
    rows, frames = flat.shape
    tmax = basis.shape[0]
    sends, wide = spread.shape
    high, rows_dev, lanes = t.shape
    span = cols * sends
    per = 2 if rows_dev % 2 == 0 else 1
    return pl.pallas_call(
        functools.partial(expand_kernel, cols, per),
        grid=(rows // (span * per),),
        in_specs=[VSPEC] * 4,
        out_specs=pl.BlockSpec((span * per, frames), lambda i: (i, 0)),
        out_shape=jax.ShapeDtypeStruct(flat.shape, F32),
        scratch_shapes=[
            VMEM((rows_dev, high, lanes), F32),
            VMEM((2, wide, span), BF16),
            VMEM((3 * tmax, frames), BF16),
        ],
        compiler_params=params(),
        name="expand",
    )(flat, t, basis, spread)


def shifted(x, axis, by, size):
    return lax.ppermute(x, axis, [(i, (i + by) % size) for i in range(size)])


def exchange_sum(x, axis, size, stride=1):
    total = x
    for by in range(stride, size, stride):
        total = total + shifted(x, axis, by, size)
    return total


def sum_all(x, rows, cols):
    x = exchange_sum(x, "col", cols)
    if rows % 2 or rows == 2:
        return exchange_sum(x, "row", rows)
    x = exchange_sum(x, "row", rows, 2)
    return x + lax.ppermute(x, "row", [(i, i ^ 1) for i in range(rows)])


def sum_halves(mine, other, rows, cols):
    pairs = [(i, i ^ 1) for i in range(rows)]
    mine = mine + lax.ppermute(other, "row", pairs)
    mine = exchange_sum(mine, "row", rows, 2)
    mine = exchange_sum(mine, "col", cols)
    return mine, lax.ppermute(mine, "row", pairs)


def local(rows, cols, signal, start_frames, start_sends, start_rows, start_cols, rank_frames, rank_sends):
    rows_dev, cols_dev, sends, frames = signal.shape
    kmax, tmax = start_sends.shape[1], start_frames.shape[1]
    devices = rows * cols
    flat = signal.reshape(-1, frames)
    side = (lax.axis_index("row") % 2).astype(jnp.int32).reshape(1)

    col = lax.axis_index("col").astype(jnp.int32).reshape(1)

    near, mine, other = signal_grams(flat, sends, side, col)
    mine, other = sum_halves(mine, other, rows, cols)
    basis, spread = small_bases(
        mine, other, side, start_frames, start_sends, rank_frames, rank_sends, cols_dev
    )

    low = min(LANES // cols_dev, kmax * tmax // devices, kmax)
    lanes = low * cols_dev
    near = in_vmem(near)
    core = project(near, basis, spread, rows_dev, cols_dev, lanes)
    groups = core.shape[0] // devices
    m = lax.all_to_all(core.reshape(rows, cols, groups, rows_dev, lanes), "row", 0, 0)

    gram_rows, *pieces = row_gram(m, col)
    pieces = [pieces[0]] + [shifted(piece, "col", by, cols) for by, piece in enumerate(pieces) if by]
    gram_rows = sum_all(gram_rows, rows, cols)
    basis_rows, second, gram_cols = second_stage(gram_rows, start_rows, col, pieces, cols_dev)
    gram_cols = sum_all(gram_cols, rows, cols)
    t = third_stage(gram_cols, start_cols, basis_rows, second, m.shape, cols_dev)

    t = t.reshape(devices, groups, rows_dev, lanes)
    t = lax.all_to_all(t, ("row", "col"), 0, 0).reshape(devices * groups, rows_dev, lanes)
    return expand(near, t, basis, spread, cols_dev).reshape(signal.shape)


def solution(mesh):
    rows, cols = mesh.shape["row"], mesh.shape["col"]
    return jax.shard_map(
        functools.partial(local, rows, cols),
        mesh=mesh,
        in_specs=(P("row", "col", None, None), P(), P(), P(), P(), P(), P()),
        out_specs=P("row", "col", None, None),
        check_vma=False,
    )
```

profile of v0, /device:TPU:0, one launch (start us, length us, event | category | flops | bytes accessed | tf_op | source)
XLA Modules:
  0.0 125.7 jit_solution(3185456871560355001)
XLA Ops:
  0.0 7.5 %signal_grams.1 = (f32[8192,256]{1,0:T(8,128)S(1)}, f32[136,128]{1,0:T(8,128)S(1)}, f32[136,128]{1,0:T(8,128)S(1)}) custom-call(f32[8192,256]{1,0:T(8,128)} %bitcast.17, s32[1]{0:T(128)} %bitcast.1.side_ref, s32[1]{0:T(128)} %bitcast.2.col_ref), custom_call_target="tpu_custom_call" | custom-call | tf_op jit(solution)/shard_map/signal_grams/pallas_call | solution.py:141
  7.5 0.6 collective-permute-start
  8.1 0.9 collective-permute-done
  9.0 3.8 %collective-permute-start.3 = (f32[136,128]{1,0:T(8,128)S(1)}, f32[136,128]{1,0:T(8,128)S(1)}, u32[]{:S(2)}, u32[]{:S(2)}) collective-permute-start(f32[136,128]{1,0:T(8,128)S(1)} %add.70), channel_id=1, source_target_pairs={{0,24},{4,28},{8,0},{12,4},{16,8},{20,12},{24,16},{28,20},{1,25},{... | collective-permute-start | bytes 208904 | tf_op jit(solution)/shard_map/ppermute | solution.py:490
  12.8 0.5 collective-permute-start.2
  13.3 0.6 collective-permute-start.1
  13.9 1.4 %collective-permute-done.3 = f32[136,128]{1,0:T(8,128)S(1)} collective-permute-done((f32[136,128]{1,0:T(8,128)S(1)}, f32[136,128]{1,0:T(8,128)S(1)}, u32[]{:S(2)}, u32[]{:S(2)}) %collective-permute-start.3) | collective-permute-done | bytes 69664 | tf_op jit(solution)/shard_map/ppermute | solution.py:490
  15.3 2.6 %collective-permute-done.2 = f32[136,128]{1,0:T(8,128)S(1)} collective-permute-done((f32[136,128]{1,0:T(8,128)S(1)}, f32[136,128]{1,0:T(8,128)S(1)}, u32[]{:S(2)}, u32[]{:S(2)}) %collective-permute-start.2) | collective-permute-done | bytes 69664 | tf_op jit(solution)/shard_map/ppermute | solution.py:490
  17.9 0.7 collective-permute-done.1
  18.7 3.6 %collective-permute-start.6 = (f32[136,128]{1,0:T(8,128)S(1)}, f32[136,128]{1,0:T(8,128)S(1)}, u32[]{:S(2)}, u32[]{:S(2)}) collective-permute-start(f32[136,128]{1,0:T(8,128)S(1)} %add_add_fusion.1), channel_id=1, source_target_pairs={{0,3},{1,0},{2,1},{3,2},{4,7},{5,4},{6,5},{7,6},{8,11},{9,8},{10,9... | collective-permute-start | bytes 208904 | tf_op jit(solution)/shard_map/ppermute | solution.py:490
  22.3 1.0 collective-permute-start.4
  23.3 0.9 collective-permute-done.6
  24.3 3.3 %collective-permute-done.5 = f32[136,128]{1,0:T(8,128)S(1)} collective-permute-done((f32[136,128]{1,0:T(8,128)S(1)}, f32[136,128]{1,0:T(8,128)S(1)}, u32[]{:S(2)}, u32[]{:S(2)}) %collective-permute-start.5) | collective-permute-done | bytes 69664 | tf_op jit(solution)/shard_map/ppermute | solution.py:490
  27.5 0.9 collective-permute-done.4
  29.9 2.9 %small_bases.1 = (f32[32,256]{1,0:T(8,128)S(1)}, f32[16,256]{1,0:T(8,128)S(1)}) custom-call(f32[136,128]{1,0:T(8,128)S(1)} %add_add_fusion.mine_ref, f32[136,128]{1,0:T(8,128)S(1)} %collective-permute-done.7.other_ref, s32[1]{0:T(128)} %bitcast.1.side_ref, f32[32,256]{1,0:T(8,128)S(1)} %bitcast.15, f32[8,128]{1,0:T(8,128)S(1)} %pad.4.ss_ref, ...), custom_call_target="tpu_custom_call" | custom-call | tf_op jit(solution)/shard_map/small_bases/pallas_call | solution.py:244
  32.7 5.9 %project.1 = f32[64,16,128]{2,1,0:T(8,128)S(1)} custom-call(f32[8192,256]{1,0:T(8,128)S(1)} %get-tuple-element.18.x_ref, f32[32,256]{1,0:T(8,128)S(1)} %get-tuple-element.21.basis_ref, f32[16,256]{1,0:T(8,128)S(1)} %get-tuple-element.22.spread_ref), custom_call_target="tpu_custom_call" | custom-call | tf_op jit(solution)/shard_map/project/pallas_call | solution.py:299
  38.6 12.3 %all_to_all.10.m_ref = f32[8,4,2,16,128]{4,3,2,1,0:T(8,128)S(1)} all-to-all(f32[8,4,2,16,128]{4,3,2,1,0:T(8,128)S(1)} %bitcast.12), channel_id=1, replica_groups=mesh['row'=8,'col'=4] {'row'}, dimensions={0} | all-to-all | bytes 1048576 | tf_op jit(solution)/shard_map/all_to_all | solution.py:536
  51.0 0.6 row_gram.1
  51.6 1.3 %collective-permute-start.10 = (f32[72,128]{1,0:T(8,128)S(1)}, f32[72,128]{1,0:T(8,128)S(1)}, u32[]{:S(2)}, u32[]{:S(2)}) collective-permute-start(f32[72,128]{1,0:T(8,128)S(1)} %get-tuple-element.23), channel_id=1, source_target_pairs={{0,3},{1,0},{2,1},{3,2},{4,7},{5,4},{6,5},{7,6},{8,11},{9,8},{10,9... | collective-permute-start | bytes 110600 | tf_op jit(solution)/shard_map/ppermute | solution.py:490
  52.9 1.9 %collective-permute-start.8 = (f32[72,128]{1,0:T(8,128)S(1)}, f32[72,128]{1,0:T(8,128)S(1)}, u32[]{:S(2)}, u32[]{:S(2)}) collective-permute-start(f32[72,128]{1,0:T(8,128)S(1)} %get-tuple-element.23), channel_id=1, source_target_pairs={{0,1},{1,2},{2,3},{3,0},{4,5},{5,6},{6,7},{7,4},{8,9},{9,10},{10,1... | collective-permute-start | bytes 110600 | tf_op jit(solution)/shard_map/ppermute | solution.py:490
  54.8 1.1 collective-permute-done.10
  56.0 2.2 %collective-permute-done.9 = f32[72,128]{1,0:T(8,128)S(1)} collective-permute-done((f32[72,128]{1,0:T(8,128)S(1)}, f32[72,128]{1,0:T(8,128)S(1)}, u32[]{:S(2)}, u32[]{:S(2)}) %collective-permute-start.9) | collective-permute-done | bytes 36896 | tf_op jit(solution)/shard_map/ppermute | solution.py:490
  58.1 0.5 collective-permute-done.8
  58.7 0.6 collective-permute-start.13
  59.3 1.5 %collective-permute-start.12 = (f32[72,128]{1,0:T(8,128)S(1)}, f32[72,128]{1,0:T(8,128)S(1)}, u32[]{:S(2)}, u32[]{:S(2)}) collective-permute-start(f32[72,128]{1,0:T(8,128)S(1)} %add_add_fusion.5), channel_id=1, source_target_pairs={{0,16},{4,20},{8,24},{12,28},{16,0},{20,4},{24,8},{28,12},{1,17},{... | collective-permute-start | bytes 110600 | tf_op jit(solution)/shard_map/ppermute | solution.py:490
  60.7 0.6 collective-permute-start.11
  61.4 1.8 %collective-permute-start.16 = (f32[8,2,16,128]{3,2,1,0:T(8,128)S(1)}, f32[8,2,16,128]{3,2,1,0:T(8,128)S(1)}, u32[]{:S(2)}, u32[]{:S(2)}) collective-permute-start(f32[8,2,16,128]{3,2,1,0:T(8,128)S(1)} %get-tuple-element.26), channel_id=1, source_target_pairs={{0,2},{1,3},{2,0},{3,1},{4,6},{5,7},{6,4},{7,5},{8,10},{9,11},{10,... | collective-permute-start | bytes 393224 | tf_op jit(solution)/shard_map/ppermute | solution.py:490
  63.2 2.1 %collective-permute-start.17 = (f32[8,2,16,128]{3,2,1,0:T(8,128)S(1)}, f32[8,2,16,128]{3,2,1,0:T(8,128)S(1)}, u32[]{:S(2)}, u32[]{:S(2)}) collective-permute-start(f32[8,2,16,128]{3,2,1,0:T(8,128)S(1)} %get-tuple-element.27), channel_id=1, source_target_pairs={{0,3},{1,0},{2,1},{3,2},{4,7},{5,4},{6,5},{7,6},{8,11},{9,8},{10,9... | collective-permute-start | bytes 393224 | tf_op jit(solution)/shard_map/ppermute | solution.py:490
  65.4 0.2 collective-permute-done.11
  65.7 1.2 collective-permute-done.14
  66.9 1.9 %collective-permute-done.15.refs_1_ = f32[8,2,16,128]{3,2,1,0:T(8,128)S(1)} collective-permute-done((f32[8,2,16,128]{3,2,1,0:T(8,128)S(1)}, f32[8,2,16,128]{3,2,1,0:T(8,128)S(1)}, u32[]{:S(2)}, u32[]{:S(2)}) %collective-permute-start.15) | collective-permute-done | bytes 131104 | tf_op jit(solution)/shard_map/ppermute | solution.py:490
  68.8 2.8 %collective-permute-done.16.refs_2_ = f32[8,2,16,128]{3,2,1,0:T(8,128)S(1)} collective-permute-done((f32[8,2,16,128]{3,2,1,0:T(8,128)S(1)}, f32[8,2,16,128]{3,2,1,0:T(8,128)S(1)}, u32[]{:S(2)}, u32[]{:S(2)}) %collective-permute-start.16) | collective-permute-done | bytes 131104 | tf_op jit(solution)/shard_map/ppermute | solution.py:490
  71.6 5.7 %second_stage.1 = (f32[64,128]{1,0:T(8,128)S(1)}, f32[8,128,64]{2,1,0:T(8,128)S(1)}, f32[72,128]{1,0:T(8,128)S(1)}) custom-call(f32[72,128]{1,0:T(8,128)S(1)} %add.83.gram_ref, f32[64,128]{1,0:T(8,128)S(1)} %bitcast.16, s32[1]{0:T(128)} %bitcast.2.col_ref, f32[8,2,16,128]{3,2,1,0:T(8,128)S(1)} %get-tuple-element.24.refs_0_, ...), custom_call_target="tpu_custom_call" | custom-call | tf_op jit(solution)/shard_map/second_stage/pallas_call | solution.py:391
  77.3 3.9 %collective-permute-start.20 = (f32[72,128]{1,0:T(8,128)S(1)}, f32[72,128]{1,0:T(8,128)S(1)}, u32[]{:S(2)}, u32[]{:S(2)}) collective-permute-start(f32[72,128]{1,0:T(8,128)S(1)} %get-tuple-element.28), channel_id=1, source_target_pairs={{0,3},{1,0},{2,1},{3,2},{4,7},{5,4},{6,5},{7,6},{8,11},{9,8},{10,9... | collective-permute-start | bytes 110600 | tf_op jit(solution)/shard_map/ppermute | solution.py:490
  81.2 0.6 collective-permute-start.18
  81.8 1.0 collective-permute-done.20
  82.8 3.2 %collective-permute-done.19 = f32[72,128]{1,0:T(8,128)S(1)} collective-permute-done((f32[72,128]{1,0:T(8,128)S(1)}, f32[72,128]{1,0:T(8,128)S(1)}, u32[]{:S(2)}, u32[]{:S(2)}) %collective-permute-start.19) | collective-permute-done | bytes 36896 | tf_op jit(solution)/shard_map/ppermute | solution.py:490
  86.0 0.9 collective-permute-done.18
  86.9 2.7 %collective-permute-start.23 = (f32[72,128]{1,0:T(8,128)S(1)}, f32[72,128]{1,0:T(8,128)S(1)}, u32[]{:S(2)}, u32[]{:S(2)}) collective-permute-start(f32[72,128]{1,0:T(8,128)S(1)} %add_add_fusion.3), channel_id=1, source_target_pairs={{0,24},{4,28},{8,0},{12,4},{16,8},{20,12},{24,16},{28,20},{1,25},{... | collective-permute-start | bytes 110600 | tf_op jit(solution)/shard_map/ppermute | solution.py:490
  89.6 0.5 collective-permute-start.22
  90.1 0.1 collective-permute-start.21
  90.3 1.0 collective-permute-done.23
  91.3 2.3 %collective-permute-done.22 = f32[72,128]{1,0:T(8,128)S(1)} collective-permute-done((f32[72,128]{1,0:T(8,128)S(1)}, f32[72,128]{1,0:T(8,128)S(1)}, u32[]{:S(2)}, u32[]{:S(2)}) %collective-permute-start.22) | collective-permute-done | bytes 36896 | tf_op jit(solution)/shard_map/ppermute | solution.py:490
  93.6 1.4 %collective-permute-done.21 = f32[72,128]{1,0:T(8,128)S(1)} collective-permute-done((f32[72,128]{1,0:T(8,128)S(1)}, f32[72,128]{1,0:T(8,128)S(1)}, u32[]{:S(2)}, u32[]{:S(2)}) %collective-permute-start.21) | collective-permute-done | bytes 36896 | tf_op jit(solution)/shard_map/ppermute | solution.py:490
  95.1 1.2 collective-permute-done.24
  96.3 5.8 %third_stage.1 = f32[8,4,2,16,128]{4,3,2,1,0:T(8,128)S(1)} custom-call(f32[72,128]{1,0:T(8,128)S(1)} %add.90.gram_ref, f32[64,128]{1,0:T(8,128)S(1)} %bitcast.14, f32[64,128]{1,0:T(8,128)S(1)} %get-tuple-element.29.basis_ref, f32[8,128,64]{2,1,0:T(8,128)S(1)} %get-tuple-element.30.second_ref), custom_call_target="tpu_custom_call" | custom-call | tf_op jit(solution)/shard_map/third_stage/pallas_call | solution.py:426
  102.1 16.5 %all_to_all.11 = f32[32,2,16,128]{3,2,1,0:T(8,128)S(1)} all-to-all(f32[32,2,16,128]{3,2,1,0:T(8,128)S(1)} %bitcast.13), channel_id=1, replica_groups=mesh['row'=8,'col'=4] {'row','col'}, dimensions={0} | all-to-all | bytes 1048576 | tf_op jit(solution)/shard_map/all_to_all | solution.py:546
  118.6 7.0 %expand.1 = f32[8192,256]{1,0:T(8,128)} custom-call(f32[8192,256]{1,0:T(8,128)S(1)} %get-tuple-element.18.x_ref, f32[64,16,128]{2,1,0:T(8,128)S(1)} %bitcast.11, f32[32,256]{1,0:T(8,128)S(1)} %get-tuple-element.21.basis_ref, f32[16,256]{1,0:T(8,128)S(1)} %get-tuple-element.22.spread_ref), custom_call_target="tpu_custom_call" | custom-call | tf_op jit(solution)/shard_map/expand/pallas_call | solution.py:473
  (29 shorter events, 0.5 us)
Async XLA Ops:
  0.0 29.8 %copy-start.3 = (f32[16,8]{0,1:T(8,128)S(1)}, f32[16,8]{0,1:T(8,128)}, u32[]{:S(2)}) copy-start(f32[16,8]{0,1:T(8,128)} %param.9) | copy-start | bytes 1540
  0.0 29.9 %copy-start.1 = (f32[256,32]{0,1:T(8,128)S(1)}, f32[256,32]{0,1:T(8,128)}, u32[]{:S(2)}) copy-start(f32[256,32]{0,1:T(8,128)} %param.8) | copy-start | bytes 98308
  0.0 71.6 %copy-start.2 = (f32[128,64]{0,1:T(8,128)S(1)}, f32[128,64]{0,1:T(8,128)}, u32[]{:S(2)}) copy-start(f32[128,64]{0,1:T(8,128)} %param.10) | copy-start | bytes 98308
  7.5 88.8 %copy-start = (f32[128,64]{0,1:T(8,128)S(1)}, f32[128,64]{0,1:T(8,128)}, u32[]{:S(2)}) copy-start(f32[128,64]{0,1:T(8,128)} %param.11) | copy-start | bytes 98308
  7.5 1.5 %collective-permute-start = (f32[136,128]{1,0:T(8,128)S(1)}, f32[136,128]{1,0:T(8,128)S(1)}, u32[]{:S(2)}, u32[]{:S(2)}) collective-permute-start(f32[136,128]{1,0:T(8,128)S(1)} %get-tuple-element.20), channel_id=1, source_target_pairs={{0,4},{4,0},{8,12},{12,8},{16,20},{20,16},{24,28},{28,24},{1,5},{5... | collective-permute-start | bytes 208904 | tf_op jit(solution)/shard_map/ppermute | solution.py:510
  9.0 6.3 %collective-permute-start.3 = (f32[136,128]{1,0:T(8,128)S(1)}, f32[136,128]{1,0:T(8,128)S(1)}, u32[]{:S(2)}, u32[]{:S(2)}) collective-permute-start(f32[136,128]{1,0:T(8,128)S(1)} %add.70), channel_id=1, source_target_pairs={{0,24},{4,28},{8,0},{12,4},{16,8},{20,12},{24,16},{28,20},{1,25},{... | collective-permute-start | bytes 208904 | tf_op jit(solution)/shard_map/ppermute | solution.py:490
  12.8 5.1 %collective-permute-start.2 = (f32[136,128]{1,0:T(8,128)S(1)}, f32[136,128]{1,0:T(8,128)S(1)}, u32[]{:S(2)}, u32[]{:S(2)}) collective-permute-start(f32[136,128]{1,0:T(8,128)S(1)} %add.70), channel_id=1, source_target_pairs={{0,16},{4,20},{8,24},{12,28},{16,0},{20,4},{24,8},{28,12},{1,17},{... | collective-permute-start | bytes 208904 | tf_op jit(solution)/shard_map/ppermute | solution.py:490
  13.3 5.3 %collective-permute-start.1 = (f32[136,128]{1,0:T(8,128)S(1)}, f32[136,128]{1,0:T(8,128)S(1)}, u32[]{:S(2)}, u32[]{:S(2)}) collective-permute-start(f32[136,128]{1,0:T(8,128)S(1)} %add.70), channel_id=1, source_target_pairs={{0,8},{4,12},{8,16},{12,20},{16,24},{20,28},{24,0},{28,4},{1,9},{5... | collective-permute-start | bytes 208904 | tf_op jit(solution)/shard_map/ppermute | solution.py:490
  18.7 5.6 %collective-permute-start.6 = (f32[136,128]{1,0:T(8,128)S(1)}, f32[136,128]{1,0:T(8,128)S(1)}, u32[]{:S(2)}, u32[]{:S(2)}) collective-permute-start(f32[136,128]{1,0:T(8,128)S(1)} %add_add_fusion.1), channel_id=1, source_target_pairs={{0,3},{1,0},{2,1},{3,2},{4,7},{5,4},{6,5},{7,6},{8,11},{9,8},{10,9... | collective-permute-start | bytes 208904 | tf_op jit(solution)/shard_map/ppermute | solution.py:490
  22.3 5.2 %collective-permute-start.5 = (f32[136,128]{1,0:T(8,128)S(1)}, f32[136,128]{1,0:T(8,128)S(1)}, u32[]{:S(2)}, u32[]{:S(2)}) collective-permute-start(f32[136,128]{1,0:T(8,128)S(1)} %add_add_fusion.1), channel_id=1, source_target_pairs={{0,2},{1,3},{2,0},{3,1},{4,6},{5,7},{6,4},{7,5},{8,10},{9,11},{10,... | collective-permute-start | bytes 208904 | tf_op jit(solution)/shard_map/ppermute | solution.py:490
  22.3 6.1 %collective-permute-start.4 = (f32[136,128]{1,0:T(8,128)S(1)}, f32[136,128]{1,0:T(8,128)S(1)}, u32[]{:S(2)}, u32[]{:S(2)}) collective-permute-start(f32[136,128]{1,0:T(8,128)S(1)} %add_add_fusion.1), channel_id=1, source_target_pairs={{0,1},{1,2},{2,3},{3,0},{4,5},{5,6},{6,7},{7,4},{8,9},{9,10},{10,1... | collective-permute-start | bytes 208904 | tf_op jit(solution)/shard_map/ppermute | solution.py:490
  28.4 1.4 %collective-permute-start.7 = (f32[136,128]{1,0:T(8,128)S(1)}, f32[136,128]{1,0:T(8,128)S(1)}, u32[]{:S(2)}, u32[]{:S(2)}) collective-permute-start(f32[136,128]{1,0:T(8,128)S(1)} %add_add_fusion.mine_ref), channel_id=1, source_target_pairs={{0,4},{4,0},{8,12},{12,8},{16,20},{20,16},{24,28},{28,24},{1,5},{5... | collective-permute-start | bytes 208904 | tf_op jit(solution)/shard_map/ppermute | solution.py:513
  51.6 4.4 %collective-permute-start.10 = (f32[72,128]{1,0:T(8,128)S(1)}, f32[72,128]{1,0:T(8,128)S(1)}, u32[]{:S(2)}, u32[]{:S(2)}) collective-permute-start(f32[72,128]{1,0:T(8,128)S(1)} %get-tuple-element.23), channel_id=1, source_target_pairs={{0,3},{1,0},{2,1},{3,2},{4,7},{5,4},{6,5},{7,6},{8,11},{9,8},{10,9... | collective-permute-start | bytes 110600 | tf_op jit(solution)/shard_map/ppermute | solution.py:490
  52.9 5.3 %collective-permute-start.9 = (f32[72,128]{1,0:T(8,128)S(1)}, f32[72,128]{1,0:T(8,128)S(1)}, u32[]{:S(2)}, u32[]{:S(2)}) collective-permute-start(f32[72,128]{1,0:T(8,128)S(1)} %get-tuple-element.23), channel_id=1, source_target_pairs={{0,2},{1,3},{2,0},{3,1},{4,6},{5,7},{6,4},{7,5},{8,10},{9,11},{10,... | collective-permute-start | bytes 110600 | tf_op jit(solution)/shard_map/ppermute | solution.py:490
  52.9 5.8 %collective-permute-start.8 = (f32[72,128]{1,0:T(8,128)S(1)}, f32[72,128]{1,0:T(8,128)S(1)}, u32[]{:S(2)}, u32[]{:S(2)}) collective-permute-start(f32[72,128]{1,0:T(8,128)S(1)} %get-tuple-element.23), channel_id=1, source_target_pairs={{0,1},{1,2},{2,3},{3,0},{4,5},{5,6},{6,7},{7,4},{8,9},{9,10},{10,1... | collective-permute-start | bytes 110600 | tf_op jit(solution)/shard_map/ppermute | solution.py:490
  58.7 4.6 %collective-permute-start.13 = (f32[72,128]{1,0:T(8,128)S(1)}, f32[72,128]{1,0:T(8,128)S(1)}, u32[]{:S(2)}, u32[]{:S(2)}) collective-permute-start(f32[72,128]{1,0:T(8,128)S(1)} %add_add_fusion.5), channel_id=1, source_target_pairs={{0,24},{4,28},{8,0},{12,4},{16,8},{20,12},{24,16},{28,20},{1,25},{... | collective-permute-start | bytes 110600 | tf_op jit(solution)/shard_map/ppermute | solution.py:490
  59.3 6.1 %collective-permute-start.12 = (f32[72,128]{1,0:T(8,128)S(1)}, f32[72,128]{1,0:T(8,128)S(1)}, u32[]{:S(2)}, u32[]{:S(2)}) collective-permute-start(f32[72,128]{1,0:T(8,128)S(1)} %add_add_fusion.5), channel_id=1, source_target_pairs={{0,16},{4,20},{8,24},{12,28},{16,0},{20,4},{24,8},{28,12},{1,17},{... | collective-permute-start | bytes 110600 | tf_op jit(solution)/shard_map/ppermute | solution.py:490
  60.7 4.9 %collective-permute-start.11 = (f32[72,128]{1,0:T(8,128)S(1)}, f32[72,128]{1,0:T(8,128)S(1)}, u32[]{:S(2)}, u32[]{:S(2)}) collective-permute-start(f32[72,128]{1,0:T(8,128)S(1)} %add_add_fusion.5), channel_id=1, source_target_pairs={{0,8},{4,12},{8,16},{12,20},{16,24},{20,28},{24,0},{28,4},{1,9},{5... | collective-permute-start | bytes 110600 | tf_op jit(solution)/shard_map/ppermute | solution.py:490
  61.3 7.5 %collective-permute-start.15 = (f32[8,2,16,128]{3,2,1,0:T(8,128)S(1)}, f32[8,2,16,128]{3,2,1,0:T(8,128)S(1)}, u32[]{:S(2)}, u32[]{:S(2)}) collective-permute-start(f32[8,2,16,128]{3,2,1,0:T(8,128)S(1)} %get-tuple-element.25), channel_id=1, source_target_pairs={{0,1},{1,2},{2,3},{3,0},{4,5},{5,6},{6,7},{7,4},{8,9},{9,10},{10,1... | collective-permute-start | bytes 393224 | tf_op jit(solution)/shard_map/ppermute | solution.py:490
  61.4 10.1 %collective-permute-start.16 = (f32[8,2,16,128]{3,2,1,0:T(8,128)S(1)}, f32[8,2,16,128]{3,2,1,0:T(8,128)S(1)}, u32[]{:S(2)}, u32[]{:S(2)}) collective-permute-start(f32[8,2,16,128]{3,2,1,0:T(8,128)S(1)} %get-tuple-element.26), channel_id=1, source_target_pairs={{0,2},{1,3},{2,0},{3,1},{4,6},{5,7},{6,4},{7,5},{8,10},{9,11},{10,... | collective-permute-start | bytes 393224 | tf_op jit(solution)/shard_map/ppermute | solution.py:490
  63.2 8.3 %collective-permute-start.17 = (f32[8,2,16,128]{3,2,1,0:T(8,128)S(1)}, f32[8,2,16,128]{3,2,1,0:T(8,128)S(1)}, u32[]{:S(2)}, u32[]{:S(2)}) collective-permute-start(f32[8,2,16,128]{3,2,1,0:T(8,128)S(1)} %get-tuple-element.27), channel_id=1, source_target_pairs={{0,3},{1,0},{2,1},{3,2},{4,7},{5,4},{6,5},{7,6},{8,11},{9,8},{10,9... | collective-permute-start | bytes 393224 | tf_op jit(solution)/shard_map/ppermute | solution.py:490
  65.6 1.3 %collective-permute-start.14 = (f32[72,128]{1,0:T(8,128)S(1)}, f32[72,128]{1,0:T(8,128)S(1)}, u32[]{:S(2)}, u32[]{:S(2)}) collective-permute-start(f32[72,128]{1,0:T(8,128)S(1)} %add_add_fusion.4), channel_id=1, source_target_pairs={{0,4},{4,0},{8,12},{12,8},{16,20},{20,16},{24,28},{28,24},{1,5},{5... | collective-permute-start | bytes 110600 | tf_op jit(solution)/shard_map/ppermute | solution.py:505
  77.3 5.5 %collective-permute-start.20 = (f32[72,128]{1,0:T(8,128)S(1)}, f32[72,128]{1,0:T(8,128)S(1)}, u32[]{:S(2)}, u32[]{:S(2)}) collective-permute-start(f32[72,128]{1,0:T(8,128)S(1)} %get-tuple-element.28), channel_id=1, source_target_pairs={{0,3},{1,0},{2,1},{3,2},{4,7},{5,4},{6,5},{7,6},{8,11},{9,8},{10,9... | collective-permute-start | bytes 110600 | tf_op jit(solution)/shard_map/ppermute | solution.py:490
  81.1 4.9 %collective-permute-start.19 = (f32[72,128]{1,0:T(8,128)S(1)}, f32[72,128]{1,0:T(8,128)S(1)}, u32[]{:S(2)}, u32[]{:S(2)}) collective-permute-start(f32[72,128]{1,0:T(8,128)S(1)} %get-tuple-element.28), channel_id=1, source_target_pairs={{0,2},{1,3},{2,0},{3,1},{4,6},{5,7},{6,4},{7,5},{8,10},{9,11},{10,... | collective-permute-start | bytes 110600 | tf_op jit(solution)/shard_map/ppermute | solution.py:490
  81.2 5.8 %collective-permute-start.18 = (f32[72,128]{1,0:T(8,128)S(1)}, f32[72,128]{1,0:T(8,128)S(1)}, u32[]{:S(2)}, u32[]{:S(2)}) collective-permute-start(f32[72,128]{1,0:T(8,128)S(1)} %get-tuple-element.28), channel_id=1, source_target_pairs={{0,1},{1,2},{2,3},{3,0},{4,5},{5,6},{6,7},{7,4},{8,9},{9,10},{10,1... | collective-permute-start | bytes 110600 | tf_op jit(solution)/shard_map/ppermute | solution.py:490
  86.9 4.4 %collective-permute-start.23 = (f32[72,128]{1,0:T(8,128)S(1)}, f32[72,128]{1,0:T(8,128)S(1)}, u32[]{:S(2)}, u32[]{:S(2)}) collective-permute-start(f32[72,128]{1,0:T(8,128)S(1)} %add_add_fusion.3), channel_id=1, source_target_pairs={{0,24},{4,28},{8,0},{12,4},{16,8},{20,12},{24,16},{28,20},{1,25},{... | collective-permute-start | bytes 110600 | tf_op jit(solution)/shard_map/ppermute | solution.py:490
  89.6 4.0 %collective-permute-start.22 = (f32[72,128]{1,0:T(8,128)S(1)}, f32[72,128]{1,0:T(8,128)S(1)}, u32[]{:S(2)}, u32[]{:S(2)}) collective-permute-start(f32[72,128]{1,0:T(8,128)S(1)} %add_add_fusion.3), channel_id=1, source_target_pairs={{0,16},{4,20},{8,24},{12,28},{16,0},{20,4},{24,8},{28,12},{1,17},{... | collective-permute-start | bytes 110600 | tf_op jit(solution)/shard_map/ppermute | solution.py:490
  90.1 4.9 %collective-permute-start.21 = (f32[72,128]{1,0:T(8,128)S(1)}, f32[72,128]{1,0:T(8,128)S(1)}, u32[]{:S(2)}, u32[]{:S(2)}) collective-permute-start(f32[72,128]{1,0:T(8,128)S(1)} %add_add_fusion.3), channel_id=1, source_target_pairs={{0,8},{4,12},{8,16},{12,20},{16,24},{20,28},{24,0},{28,4},{1,9},{5... | collective-permute-start | bytes 110600 | tf_op jit(solution)/shard_map/ppermute | solution.py:490
  95.0 1.3 %collective-permute-start.24 = (f32[72,128]{1,0:T(8,128)S(1)}, f32[72,128]{1,0:T(8,128)S(1)}, u32[]{:S(2)}, u32[]{:S(2)}) collective-permute-start(f32[72,128]{1,0:T(8,128)S(1)} %add_add_fusion.2), channel_id=1, source_target_pairs={{0,4},{4,0},{8,12},{12,8},{16,20},{20,16},{24,28},{28,24},{1,5},{5... | collective-permute-start | bytes 110600 | tf_op jit(solution)/shard_map/ppermute | solution.py:505
where the time goes:
time: 127 us; the launch traced here: 126 us
  Pallas kernels  35.4 us (28%)
  waiting for transfers between devices  31.7 us (25%)
  blocking collectives  28.8 us (23%)
  starting transfers between devices  28.1 us (22%)
  between operations  1.44 us (1%)
    ppermute x21, waiting for transfers between devices, shifted(): return lax.ppermute(x, axis, [(i, (i + by) % size) for i in range(size)])  28.4 us
    ppermute x21, starting transfers between devices, shifted(): return lax.ppermute(x, axis, [(i, (i + by) % size) for i in range(size)])  27.4 us
    all_to_all x1, blocking collectives, local(): lax.all_to_all(t, ('row', 'col'), 0, 0)  16.5 us
    all_to_all x1, blocking collectives, local(): lax.all_to_all(core.reshape(rows, cols, groups, rows_dev, lanes), 'row',...  12.3 us
    pallas_call x1, Pallas kernels, signal_grams(): pl.pallas_call(functools.partial(gram_kernel, sends, block, 3), in_specs=...  7.49 us
    pallas_call x1, Pallas kernels, expand(): pl.pallas_call(functools.partial(expand_kernel, cols, per), grid=(rows //...  7.03 us
    pallas_call x1, Pallas kernels, project(): pl.pallas_call(functools.partial(core_kernel, lanes, cols, per), in_specs...  5.9 us
    pallas_call x1, Pallas kernels, third_stage(): pl.pallas_call(functools.partial(third_kernel, cols), in_specs=[VSPEC] *...  5.82 us
  transfers between devices with their start and end apart: 25, of which 21 were waited for; matrix products, arithmetic and copies ran while one was open for 0% of the time, Pallas kernels for 0%

commit v1 on v0

--- a/solution.py
+++ b/solution.py
@@ -83,27 +83,24 @@
     return jnp.concatenate([top, jnp.where(lane < h, last, corner)], axis=0)
 
 
-def gram_kernel(sends, block, ahead, x_ref, side_ref, col_ref, near_ref, mine_ref, other_ref, acc_frames, acc_sends, sems):
+def gram_kernel(sends, block, x_ref, side_ref, col_ref, near_ref, mine_ref, other_ref, acc_frames, acc_sends, sems):
     frames = x_ref.shape[1]
     group = acc_sends.shape[0]
-    steps = x_ref.shape[0] // block
+    rows = x_ref.shape[0]
+    piece = rows // sems.shape[0]
 
     def copy(step):
-        at = pl.ds(pl.multiple_of(step * block, block), block)
+        at = pl.ds(pl.multiple_of(step * piece, piece), piece)
         return pltpu.make_async_copy(x_ref.at[at, :], near_ref.at[at, :], sems.at[step])
 
-    for step in range(min(ahead, steps)):
+    for step in range(rows // piece):
         copy(step).start()
     acc_frames[...] = jnp.zeros_like(acc_frames)
     acc_sends[...] = jnp.zeros_like(acc_sends)
 
     def body(step, carry):
-        copy(step).wait()
-
-        @pl.when(step + ahead < steps)
-        def _():
-            copy(step + ahead).start()
-
+        for q in range(block // piece):
+            copy(step * (block // piece) + q).wait()
         hi, lo = split2(near_ref[pl.ds(pl.multiple_of(step * block, block), block), :])
         acc_frames[...] += mm(hi, jnp.concatenate([hi, lo], axis=1), TN)
         total = acc_sends[...]
@@ -113,7 +110,7 @@
         acc_sends[...] = total
         return carry
 
-    lax.fori_loop(0, steps, body, 0)
+    lax.fori_loop(0, rows // block, body, 0)
     cross = acc_frames[:, frames:]
     body, tail = pack(acc_frames[:, :frames] + (cross + cross.T))
     cross = acc_sends[:, group:]
@@ -136,17 +133,18 @@
 
 def signal_grams(flat, sends, side, col):
     rows, frames = flat.shape
-    block = min(rows, 1024)
+    block = min(rows, 2048)
+    piece = min(rows, 512)
     shape = (frames // 2 + SUB, LANES)
     return pl.pallas_call(
-        functools.partial(gram_kernel, sends, block, 3),
+        functools.partial(gram_kernel, sends, block),
         in_specs=[pl.BlockSpec(memory_space=pltpu.HBM)] + [pl.BlockSpec(memory_space=pltpu.SMEM)] * 2,
         out_specs=[VSPEC] * 3,
         out_shape=[VMEM(flat.shape, F32)] + [jax.ShapeDtypeStruct(shape, F32)] * 2,
         scratch_shapes=[
             VMEM((frames, 2 * frames), F32),
             VMEM((LANES, 2 * LANES), F32),
-            pltpu.SemaphoreType.DMA((rows // block,)),
+            pltpu.SemaphoreType.DMA((rows // piece,)),
         ],
         compiler_params=params(),
         name="signal_grams",
@@ -433,38 +431,51 @@
     )(gram, start.T, basis, second)
 
 
-def expand_kernel(cols, per, x_ref, t_ref, basis_ref, spread_ref, out_ref, held, mix_ref, base_ref):
-    step = pl.program_id(0)
+def expand_kernel(cols, per, x_ref, t_ref, basis_ref, spread_ref, out_ref, stage, held, mix_ref, base_ref, sems):
     tmax = basis_ref.shape[0]
-
-    @pl.when(step == 0)
-    def _():
-        hi, lo = split2(mixing(spread_ref[...], cols))
-        mix_ref[0], mix_ref[1] = hi.T, lo.T
-        hi, lo = split2(basis_ref[...])
-        for q, part in enumerate((hi, lo, hi)):
-            base_ref[q * tmax : (q + 1) * tmax] = part
-        for r in range(held.shape[0]):
-            held[r] = t_ref[:, r, :]
+    hi, lo = split2(mixing(spread_ref[...], cols))
+    mix_ref[0], mix_ref[1] = hi.T, lo.T
+    hi, lo = split2(basis_ref[...])
+    for q, part in enumerate((hi, lo, hi)):
+        base_ref[q * tmax : (q + 1) * tmax] = part
+    for r in range(held.shape[0]):
+        held[r] = t_ref[:, r, :]
 
     span = mix_ref.shape[2]
-    tiles = []
-    for q in range(per):
-        t = held[step * per + q]
-        tiles.append(jnp.concatenate([t[h * tmax : (h + 1) * tmax] for h in range(t.shape[0] // tmax)], axis=1))
-    hi, lo = split2(jnp.concatenate(tiles, axis=0))
     rows = per * tmax
-    both = mm(jnp.concatenate([hi, lo], axis=0), mix_ref[0], NN)
-    zh, zl = split2(both[:rows] + (both[rows:] + mm(hi, mix_ref[1], NN)))
-    for q in range(per):
-        h, l = zh[q * tmax : (q + 1) * tmax], zl[q * tmax : (q + 1) * tmax]
-        tissue = mm(jnp.concatenate([h, h, l], axis=0), base_ref[...], TN)
-        at = pl.multiple_of((step * per + q) * span, span)
-        out_ref[q * span : (q + 1) * span] = x_ref[pl.ds(at, span), :] - tissue
+    steps = held.shape[0] // per
+
+    def copy(step):
+        at = pl.ds(pl.multiple_of(step * per * span, per * span), per * span)
+        return pltpu.make_async_copy(stage.at[at, :], out_ref.at[at, :], sems.at[step])
+
+    def body(step, carry):
+        @pl.when(step > 0)
+        def _():
+            copy(step - 1).start()
+
+        tiles = []
+        for q in range(per):
+            t = held[step * per + q]
+            tiles.append(jnp.concatenate([t[h * tmax : (h + 1) * tmax] for h in range(t.shape[0] // tmax)], axis=1))
+        hi, lo = split2(jnp.concatenate(tiles, axis=0))
+        both = mm(jnp.concatenate([hi, lo], axis=0), mix_ref[0], NN)
+        zh, zl = split2(both[:rows] + (both[rows:] + mm(hi, mix_ref[1], NN)))
+        for q in range(per):
+            h, l = zh[q * tmax : (q + 1) * tmax], zl[q * tmax : (q + 1) * tmax]
+            tissue = mm(jnp.concatenate([h, h, l], axis=0), base_ref[...], TN)
+            at = pl.multiple_of((step * per + q) * span, span)
+            stage[pl.ds(at, span), :] = x_ref[pl.ds(at, span), :] - tissue
+        return carry
+
+    lax.fori_loop(0, steps, body, 0)
+    copy(steps - 1).start()
+    for step in range(steps):
+        copy(step).wait()
 
 
 def expand(flat, t, basis, spread, cols):
-    rows, frames = flat.shape
+    frames = flat.shape[1]
     tmax = basis.shape[0]
     sends, wide = spread.shape
     high, rows_dev, lanes = t.shape
@@ -472,14 +483,15 @@
     per = 2 if rows_dev % 2 == 0 else 1
     return pl.pallas_call(
         functools.partial(expand_kernel, cols, per),
-        grid=(rows // (span * per),),
         in_specs=[VSPEC] * 4,
-        out_specs=pl.BlockSpec((span * per, frames), lambda i: (i, 0)),
+        out_specs=pl.BlockSpec(memory_space=pltpu.HBM),
         out_shape=jax.ShapeDtypeStruct(flat.shape, F32),
         scratch_shapes=[
+            VMEM(flat.shape, F32),
             VMEM((rows_dev, high, lanes), F32),
             VMEM((2, wide, span), BF16),
             VMEM((3 * tmax, frames), BF16),
+            pltpu.SemaphoreType.DMA((rows_dev // per,)),
         ],
         compiler_params=params(),
         name="expand",

time: 127 us -> 125 us (0.984)
    pallas_call x2, Pallas kernels: 14.5 us -> 13.2 us  [the longest x1 7.19 us: signal_grams(): pl.pallas_call(functools.partial(gram_kernel, sends, block), in_specs=[pl...]
where the time goes in v1:
time: 125 us; the launch traced here: 124 us
  Pallas kernels  34.2 us (27%)
  waiting for transfers between devices  31.7 us (25%)
  blocking collectives  28.8 us (23%)
  starting transfers between devices  28.1 us (22%)
  between operations  1.44 us (1%)
    ppermute x21, waiting for transfers between devices, shifted(): return lax.ppermute(x, axis, [(i, (i + by) % size) for i in range(size)])  28.4 us
    ppermute x21, starting transfers between devices, shifted(): return lax.ppermute(x, axis, [(i, (i + by) % size) for i in range(size)])  27.3 us
    all_to_all x1, blocking collectives, local(): lax.all_to_all(t, ('row', 'col'), 0, 0)  16.5 us
    all_to_all x1, blocking collectives, local(): lax.all_to_all(core.reshape(rows, cols, groups, rows_dev, lanes), 'row',...  12.3 us
    pallas_call x1, Pallas kernels, signal_grams(): pl.pallas_call(functools.partial(gram_kernel, sends, block), in_specs=[pl...  7.19 us
    pallas_call x1, Pallas kernels, expand(): pl.pallas_call(functools.partial(expand_kernel, cols, per), in_specs=[VSP...  6.06 us
    pallas_call x1, Pallas kernels, project(): pl.pallas_call(functools.partial(core_kernel, lanes, cols, per), in_specs...  5.9 us
    pallas_call x1, Pallas kernels, third_stage(): pl.pallas_call(functools.partial(third_kernel, cols), in_specs=[VSPEC] *...  5.82 us
  transfers between devices with their start and end apart: 25, of which 21 were waited for; matrix products, arithmetic and copies ran while one was open for 0% of the time, Pallas kernels for 0%

profile of v1, /device:TPU:0, one launch (start us, length us, event | category | flops | bytes accessed | tf_op | source)
XLA Modules:
  0.0 124.4 jit_solution(13981857664380618359)
XLA Ops:
  0.0 7.2 %signal_grams.1 = (f32[8192,256]{1,0:T(8,128)S(1)}, f32[136,128]{1,0:T(8,128)S(1)}, f32[136,128]{1,0:T(8,128)S(1)}) custom-call(f32[8192,256]{1,0:T(8,128)} %bitcast.17, s32[1]{0:T(128)} %bitcast.1.side_ref, s32[1]{0:T(128)} %bitcast.2.col_ref), custom_call_target="tpu_custom_call" | custom-call | tf_op jit(solution)/shard_map/signal_grams/pallas_call | solution.py:139
  7.2 0.6 collective-permute-start
  7.8 0.9 collective-permute-done
  8.7 3.8 %collective-permute-start.3 = (f32[136,128]{1,0:T(8,128)S(1)}, f32[136,128]{1,0:T(8,128)S(1)}, u32[]{:S(2)}, u32[]{:S(2)}) collective-permute-start(f32[136,128]{1,0:T(8,128)S(1)} %add.70), channel_id=1, source_target_pairs={{0,24},{4,28},{8,0},{12,4},{16,8},{20,12},{24,16},{28,20},{1,25},{... | collective-permute-start | bytes 208904 | tf_op jit(solution)/shard_map/ppermute | solution.py:502
  12.5 0.5 collective-permute-start.2
  13.0 0.6 collective-permute-start.1
  13.6 1.4 %collective-permute-done.3 = f32[136,128]{1,0:T(8,128)S(1)} collective-permute-done((f32[136,128]{1,0:T(8,128)S(1)}, f32[136,128]{1,0:T(8,128)S(1)}, u32[]{:S(2)}, u32[]{:S(2)}) %collective-permute-start.3) | collective-permute-done | bytes 69664 | tf_op jit(solution)/shard_map/ppermute | solution.py:502
  15.0 2.6 %collective-permute-done.2 = f32[136,128]{1,0:T(8,128)S(1)} collective-permute-done((f32[136,128]{1,0:T(8,128)S(1)}, f32[136,128]{1,0:T(8,128)S(1)}, u32[]{:S(2)}, u32[]{:S(2)}) %collective-permute-start.2) | collective-permute-done | bytes 69664 | tf_op jit(solution)/shard_map/ppermute | solution.py:502
  17.6 0.7 collective-permute-done.1
  18.4 3.7 %collective-permute-start.6 = (f32[136,128]{1,0:T(8,128)S(1)}, f32[136,128]{1,0:T(8,128)S(1)}, u32[]{:S(2)}, u32[]{:S(2)}) collective-permute-start(f32[136,128]{1,0:T(8,128)S(1)} %add_add_fusion.1), channel_id=1, source_target_pairs={{0,3},{1,0},{2,1},{3,2},{4,7},{5,4},{6,5},{7,6},{8,11},{9,8},{10,9... | collective-permute-start | bytes 208904 | tf_op jit(solution)/shard_map/ppermute | solution.py:502
  22.0 1.0 collective-permute-start.4
  23.0 0.9 collective-permute-done.6
  24.0 3.3 %collective-permute-done.5 = f32[136,128]{1,0:T(8,128)S(1)} collective-permute-done((f32[136,128]{1,0:T(8,128)S(1)}, f32[136,128]{1,0:T(8,128)S(1)}, u32[]{:S(2)}, u32[]{:S(2)}) %collective-permute-start.5) | collective-permute-done | bytes 69664 | tf_op jit(solution)/shard_map/ppermute | solution.py:502
  27.2 0.9 collective-permute-done.4
  29.6 2.9 %small_bases.1 = (f32[32,256]{1,0:T(8,128)S(1)}, f32[16,256]{1,0:T(8,128)S(1)}) custom-call(f32[136,128]{1,0:T(8,128)S(1)} %add_add_fusion.mine_ref, f32[136,128]{1,0:T(8,128)S(1)} %collective-permute-done.7.other_ref, s32[1]{0:T(128)} %bitcast.1.side_ref, f32[32,256]{1,0:T(8,128)S(1)} %bitcast.15, f32[8,128]{1,0:T(8,128)S(1)} %pad.4.ss_ref, ...), custom_call_target="tpu_custom_call" | custom-call | tf_op jit(solution)/shard_map/small_bases/pallas_call | solution.py:242
  32.4 5.9 %project.1 = f32[64,16,128]{2,1,0:T(8,128)S(1)} custom-call(f32[8192,256]{1,0:T(8,128)S(1)} %get-tuple-element.18.x_ref, f32[32,256]{1,0:T(8,128)S(1)} %get-tuple-element.21.basis_ref, f32[16,256]{1,0:T(8,128)S(1)} %get-tuple-element.22.spread_ref), custom_call_target="tpu_custom_call" | custom-call | tf_op jit(solution)/shard_map/project/pallas_call | solution.py:297
  38.4 12.3 %all_to_all.10.m_ref = f32[8,4,2,16,128]{4,3,2,1,0:T(8,128)S(1)} all-to-all(f32[8,4,2,16,128]{4,3,2,1,0:T(8,128)S(1)} %bitcast.12), channel_id=1, replica_groups=mesh['row'=8,'col'=4] {'row'}, dimensions={0} | all-to-all | bytes 1048576 | tf_op jit(solution)/shard_map/all_to_all | solution.py:548
  50.7 0.6 row_gram.1
  51.3 1.3 %collective-permute-start.10 = (f32[72,128]{1,0:T(8,128)S(1)}, f32[72,128]{1,0:T(8,128)S(1)}, u32[]{:S(2)}, u32[]{:S(2)}) collective-permute-start(f32[72,128]{1,0:T(8,128)S(1)} %get-tuple-element.23), channel_id=1, source_target_pairs={{0,3},{1,0},{2,1},{3,2},{4,7},{5,4},{6,5},{7,6},{8,11},{9,8},{10,9... | collective-permute-start | bytes 110600 | tf_op jit(solution)/shard_map/ppermute | solution.py:502
  52.6 1.9 %collective-permute-start.8 = (f32[72,128]{1,0:T(8,128)S(1)}, f32[72,128]{1,0:T(8,128)S(1)}, u32[]{:S(2)}, u32[]{:S(2)}) collective-permute-start(f32[72,128]{1,0:T(8,128)S(1)} %get-tuple-element.23), channel_id=1, source_target_pairs={{0,1},{1,2},{2,3},{3,0},{4,5},{5,6},{6,7},{7,4},{8,9},{9,10},{10,1... | collective-permute-start | bytes 110600 | tf_op jit(solution)/shard_map/ppermute | solution.py:502
  54.5 1.2 collective-permute-done.10
  55.7 2.2 %collective-permute-done.9 = f32[72,128]{1,0:T(8,128)S(1)} collective-permute-done((f32[72,128]{1,0:T(8,128)S(1)}, f32[72,128]{1,0:T(8,128)S(1)}, u32[]{:S(2)}, u32[]{:S(2)}) %collective-permute-start.9) | collective-permute-done | bytes 36896 | tf_op jit(solution)/shard_map/ppermute | solution.py:502
  57.9 0.5 collective-permute-done.8
  58.4 0.6 collective-permute-start.13
  59.0 1.5 %collective-permute-start.12 = (f32[72,128]{1,0:T(8,128)S(1)}, f32[72,128]{1,0:T(8,128)S(1)}, u32[]{:S(2)}, u32[]{:S(2)}) collective-permute-start(f32[72,128]{1,0:T(8,128)S(1)} %add_add_fusion.5), channel_id=1, source_target_pairs={{0,16},{4,20},{8,24},{12,28},{16,0},{20,4},{24,8},{28,12},{1,17},{... | collective-permute-start | bytes 110600 | tf_op jit(solution)/shard_map/ppermute | solution.py:502
  60.5 0.6 collective-permute-start.11
  61.1 1.8 %collective-permute-start.16 = (f32[8,2,16,128]{3,2,1,0:T(8,128)S(1)}, f32[8,2,16,128]{3,2,1,0:T(8,128)S(1)}, u32[]{:S(2)}, u32[]{:S(2)}) collective-permute-start(f32[8,2,16,128]{3,2,1,0:T(8,128)S(1)} %get-tuple-element.26), channel_id=1, source_target_pairs={{0,2},{1,3},{2,0},{3,1},{4,6},{5,7},{6,4},{7,5},{8,10},{9,11},{10,... | collective-permute-start | bytes 393224 | tf_op jit(solution)/shard_map/ppermute | solution.py:502
  62.9 2.1 %collective-permute-start.17 = (f32[8,2,16,128]{3,2,1,0:T(8,128)S(1)}, f32[8,2,16,128]{3,2,1,0:T(8,128)S(1)}, u32[]{:S(2)}, u32[]{:S(2)}) collective-permute-start(f32[8,2,16,128]{3,2,1,0:T(8,128)S(1)} %get-tuple-element.27), channel_id=1, source_target_pairs={{0,3},{1,0},{2,1},{3,2},{4,7},{5,4},{6,5},{7,6},{8,11},{9,8},{10,9... | collective-permute-start | bytes 393224 | tf_op jit(solution)/shard_map/ppermute | solution.py:502
  65.1 0.2 collective-permute-done.11
  65.4 1.2 collective-permute-done.14
  66.6 1.9 %collective-permute-done.15.refs_1_ = f32[8,2,16,128]{3,2,1,0:T(8,128)S(1)} collective-permute-done((f32[8,2,16,128]{3,2,1,0:T(8,128)S(1)}, f32[8,2,16,128]{3,2,1,0:T(8,128)S(1)}, u32[]{:S(2)}, u32[]{:S(2)}) %collective-permute-start.15) | collective-permute-done | bytes 131104 | tf_op jit(solution)/shard_map/ppermute | solution.py:502
  68.5 2.8 %collective-permute-done.16.refs_2_ = f32[8,2,16,128]{3,2,1,0:T(8,128)S(1)} collective-permute-done((f32[8,2,16,128]{3,2,1,0:T(8,128)S(1)}, f32[8,2,16,128]{3,2,1,0:T(8,128)S(1)}, u32[]{:S(2)}, u32[]{:S(2)}) %collective-permute-start.16) | collective-permute-done | bytes 131104 | tf_op jit(solution)/shard_map/ppermute | solution.py:502
  71.3 5.7 %second_stage.1 = (f32[64,128]{1,0:T(8,128)S(1)}, f32[8,128,64]{2,1,0:T(8,128)S(1)}, f32[72,128]{1,0:T(8,128)S(1)}) custom-call(f32[72,128]{1,0:T(8,128)S(1)} %add.83.gram_ref, f32[64,128]{1,0:T(8,128)S(1)} %bitcast.16, s32[1]{0:T(128)} %bitcast.2.col_ref, f32[8,2,16,128]{3,2,1,0:T(8,128)S(1)} %get-tuple-element.24.refs_0_, ...), custom_call_target="tpu_custom_call" | custom-call | tf_op jit(solution)/shard_map/second_stage/pallas_call | solution.py:389
  77.0 3.9 %collective-permute-start.20 = (f32[72,128]{1,0:T(8,128)S(1)}, f32[72,128]{1,0:T(8,128)S(1)}, u32[]{:S(2)}, u32[]{:S(2)}) collective-permute-start(f32[72,128]{1,0:T(8,128)S(1)} %get-tuple-element.28), channel_id=1, source_target_pairs={{0,3},{1,0},{2,1},{3,2},{4,7},{5,4},{6,5},{7,6},{8,11},{9,8},{10,9... | collective-permute-start | bytes 110600 | tf_op jit(solution)/shard_map/ppermute | solution.py:502
  80.9 0.6 collective-permute-start.18
  81.5 1.0 collective-permute-done.20
  82.5 3.2 %collective-permute-done.19 = f32[72,128]{1,0:T(8,128)S(1)} collective-permute-done((f32[72,128]{1,0:T(8,128)S(1)}, f32[72,128]{1,0:T(8,128)S(1)}, u32[]{:S(2)}, u32[]{:S(2)}) %collective-permute-start.19) | collective-permute-done | bytes 36896 | tf_op jit(solution)/shard_map/ppermute | solution.py:502
  85.7 0.9 collective-permute-done.18
  86.6 2.7 %collective-permute-start.23 = (f32[72,128]{1,0:T(8,128)S(1)}, f32[72,128]{1,0:T(8,128)S(1)}, u32[]{:S(2)}, u32[]{:S(2)}) collective-permute-start(f32[72,128]{1,0:T(8,128)S(1)} %add_add_fusion.3), channel_id=1, source_target_pairs={{0,24},{4,28},{8,0},{12,4},{16,8},{20,12},{24,16},{28,20},{1,25},{... | collective-permute-start | bytes 110600 | tf_op jit(solution)/shard_map/ppermute | solution.py:502
  89.3 0.5 collective-permute-start.22
  89.8 0.1 collective-permute-start.21
  90.0 1.0 collective-permute-done.23
  91.0 2.3 %collective-permute-done.22 = f32[72,128]{1,0:T(8,128)S(1)} collective-permute-done((f32[72,128]{1,0:T(8,128)S(1)}, f32[72,128]{1,0:T(8,128)S(1)}, u32[]{:S(2)}, u32[]{:S(2)}) %collective-permute-start.22) | collective-permute-done | bytes 36896 | tf_op jit(solution)/shard_map/ppermute | solution.py:502
  93.3 1.4 %collective-permute-done.21 = f32[72,128]{1,0:T(8,128)S(1)} collective-permute-done((f32[72,128]{1,0:T(8,128)S(1)}, f32[72,128]{1,0:T(8,128)S(1)}, u32[]{:S(2)}, u32[]{:S(2)}) %collective-permute-start.21) | collective-permute-done | bytes 36896 | tf_op jit(solution)/shard_map/ppermute | solution.py:502
  94.8 1.2 collective-permute-done.24
  96.0 5.8 %third_stage.1 = f32[8,4,2,16,128]{4,3,2,1,0:T(8,128)S(1)} custom-call(f32[72,128]{1,0:T(8,128)S(1)} %add.90.gram_ref, f32[64,128]{1,0:T(8,128)S(1)} %bitcast.14, f32[64,128]{1,0:T(8,128)S(1)} %get-tuple-element.29.basis_ref, f32[8,128,64]{2,1,0:T(8,128)S(1)} %get-tuple-element.30.second_ref), custom_call_target="tpu_custom_call" | custom-call | tf_op jit(solution)/shard_map/third_stage/pallas_call | solution.py:424
  101.8 16.5 %all_to_all.11 = f32[32,2,16,128]{3,2,1,0:T(8,128)S(1)} all-to-all(f32[32,2,16,128]{3,2,1,0:T(8,128)S(1)} %bitcast.13), channel_id=1, replica_groups=mesh['row'=8,'col'=4] {'row','col'}, dimensions={0} | all-to-all | bytes 1048576 | tf_op jit(solution)/shard_map/all_to_all | solution.py:558
  118.3 6.1 %expand.1 = f32[8192,256]{1,0:T(8,128)} custom-call(f32[8192,256]{1,0:T(8,128)S(1)} %get-tuple-element.18.x_ref, f32[64,16,128]{2,1,0:T(8,128)S(1)} %bitcast.11, f32[32,256]{1,0:T(8,128)S(1)} %get-tuple-element.21.basis_ref, f32[16,256]{1,0:T(8,128)S(1)} %get-tuple-element.22.spread_ref), custom_call_target="tpu_custom_call" | custom-call | tf_op jit(solution)/shard_map/expand/pallas_call | solution.py:484
  (29 shorter events, 0.5 us)
Async XLA Ops:
  0.0 29.5 %copy-start.3 = (f32[16,8]{0,1:T(8,128)S(1)}, f32[16,8]{0,1:T(8,128)}, u32[]{:S(2)}) copy-start(f32[16,8]{0,1:T(8,128)} %param.9) | copy-start | bytes 1540
  0.0 29.6 %copy-start.1 = (f32[256,32]{0,1:T(8,128)S(1)}, f32[256,32]{0,1:T(8,128)}, u32[]{:S(2)}) copy-start(f32[256,32]{0,1:T(8,128)} %param.8) | copy-start | bytes 98308
  0.0 71.3 %copy-start.2 = (f32[128,64]{0,1:T(8,128)S(1)}, f32[128,64]{0,1:T(8,128)}, u32[]{:S(2)}) copy-start(f32[128,64]{0,1:T(8,128)} %param.10) | copy-start | bytes 98308
  7.2 88.8 %copy-start = (f32[128,64]{0,1:T(8,128)S(1)}, f32[128,64]{0,1:T(8,128)}, u32[]{:S(2)}) copy-start(f32[128,64]{0,1:T(8,128)} %param.11) | copy-start | bytes 98308
  7.2 1.5 %collective-permute-start = (f32[136,128]{1,0:T(8,128)S(1)}, f32[136,128]{1,0:T(8,128)S(1)}, u32[]{:S(2)}, u32[]{:S(2)}) collective-permute-start(f32[136,128]{1,0:T(8,128)S(1)} %get-tuple-element.20), channel_id=1, source_target_pairs={{0,4},{4,0},{8,12},{12,8},{16,20},{20,16},{24,28},{28,24},{1,5},{5... | collective-permute-start | bytes 208904 | tf_op jit(solution)/shard_map/ppermute | solution.py:522
  8.7 6.3 %collective-permute-start.3 = (f32[136,128]{1,0:T(8,128)S(1)}, f32[136,128]{1,0:T(8,128)S(1)}, u32[]{:S(2)}, u32[]{:S(2)}) collective-permute-start(f32[136,128]{1,0:T(8,128)S(1)} %add.70), channel_id=1, source_target_pairs={{0,24},{4,28},{8,0},{12,4},{16,8},{20,12},{24,16},{28,20},{1,25},{... | collective-permute-start | bytes 208904 | tf_op jit(solution)/shard_map/ppermute | solution.py:502
  12.5 5.1 %collective-permute-start.2 = (f32[136,128]{1,0:T(8,128)S(1)}, f32[136,128]{1,0:T(8,128)S(1)}, u32[]{:S(2)}, u32[]{:S(2)}) collective-permute-start(f32[136,128]{1,0:T(8,128)S(1)} %add.70), channel_id=1, source_target_pairs={{0,16},{4,20},{8,24},{12,28},{16,0},{20,4},{24,8},{28,12},{1,17},{... | collective-permute-start | bytes 208904 | tf_op jit(solution)/shard_map/ppermute | solution.py:502
  13.0 5.3 %collective-permute-start.1 = (f32[136,128]{1,0:T(8,128)S(1)}, f32[136,128]{1,0:T(8,128)S(1)}, u32[]{:S(2)}, u32[]{:S(2)}) collective-permute-start(f32[136,128]{1,0:T(8,128)S(1)} %add.70), channel_id=1, source_target_pairs={{0,8},{4,12},{8,16},{12,20},{16,24},{20,28},{24,0},{28,4},{1,9},{5... | collective-permute-start | bytes 208904 | tf_op jit(solution)/shard_map/ppermute | solution.py:502
  18.4 5.6 %collective-permute-start.6 = (f32[136,128]{1,0:T(8,128)S(1)}, f32[136,128]{1,0:T(8,128)S(1)}, u32[]{:S(2)}, u32[]{:S(2)}) collective-permute-start(f32[136,128]{1,0:T(8,128)S(1)} %add_add_fusion.1), channel_id=1, source_target_pairs={{0,3},{1,0},{2,1},{3,2},{4,7},{5,4},{6,5},{7,6},{8,11},{9,8},{10,9... | collective-permute-start | bytes 208904 | tf_op jit(solution)/shard_map/ppermute | solution.py:502
  22.0 5.2 %collective-permute-start.5 = (f32[136,128]{1,0:T(8,128)S(1)}, f32[136,128]{1,0:T(8,128)S(1)}, u32[]{:S(2)}, u32[]{:S(2)}) collective-permute-start(f32[136,128]{1,0:T(8,128)S(1)} %add_add_fusion.1), channel_id=1, source_target_pairs={{0,2},{1,3},{2,0},{3,1},{4,6},{5,7},{6,4},{7,5},{8,10},{9,11},{10,... | collective-permute-start | bytes 208904 | tf_op jit(solution)/shard_map/ppermute | solution.py:502
  22.0 6.1 %collective-permute-start.4 = (f32[136,128]{1,0:T(8,128)S(1)}, f32[136,128]{1,0:T(8,128)S(1)}, u32[]{:S(2)}, u32[]{:S(2)}) collective-permute-start(f32[136,128]{1,0:T(8,128)S(1)} %add_add_fusion.1), channel_id=1, source_target_pairs={{0,1},{1,2},{2,3},{3,0},{4,5},{5,6},{6,7},{7,4},{8,9},{9,10},{10,1... | collective-permute-start | bytes 208904 | tf_op jit(solution)/shard_map/ppermute | solution.py:502
  28.1 1.4 %collective-permute-start.7 = (f32[136,128]{1,0:T(8,128)S(1)}, f32[136,128]{1,0:T(8,128)S(1)}, u32[]{:S(2)}, u32[]{:S(2)}) collective-permute-start(f32[136,128]{1,0:T(8,128)S(1)} %add_add_fusion.mine_ref), channel_id=1, source_target_pairs={{0,4},{4,0},{8,12},{12,8},{16,20},{20,16},{24,28},{28,24},{1,5},{5... | collective-permute-start | bytes 208904 | tf_op jit(solution)/shard_map/ppermute | solution.py:525
  51.3 4.4 %collective-permute-start.10 = (f32[72,128]{1,0:T(8,128)S(1)}, f32[72,128]{1,0:T(8,128)S(1)}, u32[]{:S(2)}, u32[]{:S(2)}) collective-permute-start(f32[72,128]{1,0:T(8,128)S(1)} %get-tuple-element.23), channel_id=1, source_target_pairs={{0,3},{1,0},{2,1},{3,2},{4,7},{5,4},{6,5},{7,6},{8,11},{9,8},{10,9... | collective-permute-start | bytes 110600 | tf_op jit(solution)/shard_map/ppermute | solution.py:502
  52.6 5.3 %collective-permute-start.9 = (f32[72,128]{1,0:T(8,128)S(1)}, f32[72,128]{1,0:T(8,128)S(1)}, u32[]{:S(2)}, u32[]{:S(2)}) collective-permute-start(f32[72,128]{1,0:T(8,128)S(1)} %get-tuple-element.23), channel_id=1, source_target_pairs={{0,2},{1,3},{2,0},{3,1},{4,6},{5,7},{6,4},{7,5},{8,10},{9,11},{10,... | collective-permute-start | bytes 110600 | tf_op jit(solution)/shard_map/ppermute | solution.py:502
  52.6 5.8 %collective-permute-start.8 = (f32[72,128]{1,0:T(8,128)S(1)}, f32[72,128]{1,0:T(8,128)S(1)}, u32[]{:S(2)}, u32[]{:S(2)}) collective-permute-start(f32[72,128]{1,0:T(8,128)S(1)} %get-tuple-element.23), channel_id=1, source_target_pairs={{0,1},{1,2},{2,3},{3,0},{4,5},{5,6},{6,7},{7,4},{8,9},{9,10},{10,1... | collective-permute-start | bytes 110600 | tf_op jit(solution)/shard_map/ppermute | solution.py:502
  58.4 4.6 %collective-permute-start.13 = (f32[72,128]{1,0:T(8,128)S(1)}, f32[72,128]{1,0:T(8,128)S(1)}, u32[]{:S(2)}, u32[]{:S(2)}) collective-permute-start(f32[72,128]{1,0:T(8,128)S(1)} %add_add_fusion.5), channel_id=1, source_target_pairs={{0,24},{4,28},{8,0},{12,4},{16,8},{20,12},{24,16},{28,20},{1,25},{... | collective-permute-start | bytes 110600 | tf_op jit(solution)/shard_map/ppermute | solution.py:502
  59.0 6.1 %collective-permute-start.12 = (f32[72,128]{1,0:T(8,128)S(1)}, f32[72,128]{1,0:T(8,128)S(1)}, u32[]{:S(2)}, u32[]{:S(2)}) collective-permute-start(f32[72,128]{1,0:T(8,128)S(1)} %add_add_fusion.5), channel_id=1, source_target_pairs={{0,16},{4,20},{8,24},{12,28},{16,0},{20,4},{24,8},{28,12},{1,17},{... | collective-permute-start | bytes 110600 | tf_op jit(solution)/shard_map/ppermute | solution.py:502
  60.5 4.9 %collective-permute-start.11 = (f32[72,128]{1,0:T(8,128)S(1)}, f32[72,128]{1,0:T(8,128)S(1)}, u32[]{:S(2)}, u32[]{:S(2)}) collective-permute-start(f32[72,128]{1,0:T(8,128)S(1)} %add_add_fusion.5), channel_id=1, source_target_pairs={{0,8},{4,12},{8,16},{12,20},{16,24},{20,28},{24,0},{28,4},{1,9},{5... | collective-permute-start | bytes 110600 | tf_op jit(solution)/shard_map/ppermute | solution.py:502
  61.0 7.5 %collective-permute-start.15 = (f32[8,2,16,128]{3,2,1,0:T(8,128)S(1)}, f32[8,2,16,128]{3,2,1,0:T(8,128)S(1)}, u32[]{:S(2)}, u32[]{:S(2)}) collective-permute-start(f32[8,2,16,128]{3,2,1,0:T(8,128)S(1)} %get-tuple-element.25), channel_id=1, source_target_pairs={{0,1},{1,2},{2,3},{3,0},{4,5},{5,6},{6,7},{7,4},{8,9},{9,10},{10,1... | collective-permute-start | bytes 393224 | tf_op jit(solution)/shard_map/ppermute | solution.py:502
  61.1 10.1 %collective-permute-start.16 = (f32[8,2,16,128]{3,2,1,0:T(8,128)S(1)}, f32[8,2,16,128]{3,2,1,0:T(8,128)S(1)}, u32[]{:S(2)}, u32[]{:S(2)}) collective-permute-start(f32[8,2,16,128]{3,2,1,0:T(8,128)S(1)} %get-tuple-element.26), channel_id=1, source_target_pairs={{0,2},{1,3},{2,0},{3,1},{4,6},{5,7},{6,4},{7,5},{8,10},{9,11},{10,... | collective-permute-start | bytes 393224 | tf_op jit(solution)/shard_map/ppermute | solution.py:502
  62.9 8.3 %collective-permute-start.17 = (f32[8,2,16,128]{3,2,1,0:T(8,128)S(1)}, f32[8,2,16,128]{3,2,1,0:T(8,128)S(1)}, u32[]{:S(2)}, u32[]{:S(2)}) collective-permute-start(f32[8,2,16,128]{3,2,1,0:T(8,128)S(1)} %get-tuple-element.27), channel_id=1, source_target_pairs={{0,3},{1,0},{2,1},{3,2},{4,7},{5,4},{6,5},{7,6},{8,11},{9,8},{10,9... | collective-permute-start | bytes 393224 | tf_op jit(solution)/shard_map/ppermute | solution.py:502
  65.3 1.3 %collective-permute-start.14 = (f32[72,128]{1,0:T(8,128)S(1)}, f32[72,128]{1,0:T(8,128)S(1)}, u32[]{:S(2)}, u32[]{:S(2)}) collective-permute-start(f32[72,128]{1,0:T(8,128)S(1)} %add_add_fusion.4), channel_id=1, source_target_pairs={{0,4},{4,0},{8,12},{12,8},{16,20},{20,16},{24,28},{28,24},{1,5},{5... | collective-permute-start | bytes 110600 | tf_op jit(solution)/shard_map/ppermute | solution.py:517
  77.0 5.5 %collective-permute-start.20 = (f32[72,128]{1,0:T(8,128)S(1)}, f32[72,128]{1,0:T(8,128)S(1)}, u32[]{:S(2)}, u32[]{:S(2)}) collective-permute-start(f32[72,128]{1,0:T(8,128)S(1)} %get-tuple-element.28), channel_id=1, source_target_pairs={{0,3},{1,0},{2,1},{3,2},{4,7},{5,4},{6,5},{7,6},{8,11},{9,8},{10,9... | collective-permute-start | bytes 110600 | tf_op jit(solution)/shard_map/ppermute | solution.py:502
  80.9 4.9 %collective-permute-start.19 = (f32[72,128]{1,0:T(8,128)S(1)}, f32[72,128]{1,0:T(8,128)S(1)}, u32[]{:S(2)}, u32[]{:S(2)}) collective-permute-start(f32[72,128]{1,0:T(8,128)S(1)} %get-tuple-element.28), channel_id=1, source_target_pairs={{0,2},{1,3},{2,0},{3,1},{4,6},{5,7},{6,4},{7,5},{8,10},{9,11},{10,... | collective-permute-start | bytes 110600 | tf_op jit(solution)/shard_map/ppermute | solution.py:502
  80.9 5.8 %collective-permute-start.18 = (f32[72,128]{1,0:T(8,128)S(1)}, f32[72,128]{1,0:T(8,128)S(1)}, u32[]{:S(2)}, u32[]{:S(2)}) collective-permute-start(f32[72,128]{1,0:T(8,128)S(1)} %get-tuple-element.28), channel_id=1, source_target_pairs={{0,1},{1,2},{2,3},{3,0},{4,5},{5,6},{6,7},{7,4},{8,9},{9,10},{10,1... | collective-permute-start | bytes 110600 | tf_op jit(solution)/shard_map/ppermute | solution.py:502
  86.6 4.4 %collective-permute-start.23 = (f32[72,128]{1,0:T(8,128)S(1)}, f32[72,128]{1,0:T(8,128)S(1)}, u32[]{:S(2)}, u32[]{:S(2)}) collective-permute-start(f32[72,128]{1,0:T(8,128)S(1)} %add_add_fusion.3), channel_id=1, source_target_pairs={{0,24},{4,28},{8,0},{12,4},{16,8},{20,12},{24,16},{28,20},{1,25},{... | collective-permute-start | bytes 110600 | tf_op jit(solution)/shard_map/ppermute | solution.py:502
  89.3 4.0 %collective-permute-start.22 = (f32[72,128]{1,0:T(8,128)S(1)}, f32[72,128]{1,0:T(8,128)S(1)}, u32[]{:S(2)}, u32[]{:S(2)}) collective-permute-start(f32[72,128]{1,0:T(8,128)S(1)} %add_add_fusion.3), channel_id=1, source_target_pairs={{0,16},{4,20},{8,24},{12,28},{16,0},{20,4},{24,8},{28,12},{1,17},{... | collective-permute-start | bytes 110600 | tf_op jit(solution)/shard_map/ppermute | solution.py:502
  89.8 4.9 %collective-permute-start.21 = (f32[72,128]{1,0:T(8,128)S(1)}, f32[72,128]{1,0:T(8,128)S(1)}, u32[]{:S(2)}, u32[]{:S(2)}) collective-permute-start(f32[72,128]{1,0:T(8,128)S(1)} %add_add_fusion.3), channel_id=1, source_target_pairs={{0,8},{4,12},{8,16},{12,20},{16,24},{20,28},{24,0},{28,4},{1,9},{5... | collective-permute-start | bytes 110600 | tf_op jit(solution)/shard_map/ppermute | solution.py:502
  94.7 1.3 %collective-permute-start.24 = (f32[72,128]{1,0:T(8,128)S(1)}, f32[72,128]{1,0:T(8,128)S(1)}, u32[]{:S(2)}, u32[]{:S(2)}) collective-permute-start(f32[72,128]{1,0:T(8,128)S(1)} %add_add_fusion.2), channel_id=1, source_target_pairs={{0,4},{4,0},{8,12},{12,8},{16,20},{20,16},{24,28},{28,24},{1,5},{5... | collective-permute-start | bytes 110600 | tf_op jit(solution)/shard_map/ppermute | solution.py:517
